TPU v7x, 32 devices: a whole 2x2x4 slice. The times are simulated.
32 devices in a mesh: pq: 8 (over z, x), hh: 4 (over y, core).
Axes of the slice: x: 2, y: 2, z: 4, core: 2. Of those that a mesh axis runs over, the one named last changes fastest.
Arguments:
- amplitudes: bfloat16 [4096, 2048], P('hh', 'pq'), may hold values from -6 to 6
- integrals: bfloat16 [4096, 2048], P('hh', 'pq'), may hold values from -0.001953125 to 0.001953125
- left_amps: bfloat16 [8, 4096, 1024], P(None, 'hh', 'pq'), may hold values from -6 to 6
Outputs:
- sigma_ladder: bfloat16 [8, 4096, 1024], P(None, 'hh', 'pq')
- subspace: float32 [8, 8], replicated
All inputs are finite; a program needn't handle non-finite values.
Results may differ from a plain program's by a relative error of at most 0.0049.
Values may be sent and summed in bfloat16 or wider, within the bound.
No kernel may reach another device: no remote copies, remote signals or barrier semaphores. Data moves between devices by JAX's collectives and lax.ppermute only.
A program may use at most 64 MiB of HBM per device.

v0:
```python
import math
import jax
import jax.numpy as jnp
from jax import lax
from jax.sharding import PartitionSpec as P

OCC_PAIRS = 4096


def body(amplitudes, integrals, left_amps):
    root_count = left_amps.shape[0]
    ab_cols = left_amps.shape[2]
    partial_t = lax.dot_general(
        integrals,
        lax.all_gather(amplitudes, "hh", axis=0, tiled=True),
        (((1,), (1,)), ((), ())),
        preferred_element_type=jnp.float32,
    )
    ladder_t = lax.psum_scatter(partial_t, "pq", scatter_dimension=1, tiled=True).astype(
        jnp.bfloat16
    )
    ladder_t = lax.all_gather(ladder_t, "pq", axis=1, tiled=True)
    rows_out = lax.dot_general(
        ladder_t,
        lax.all_gather(left_amps, "hh", axis=1, tiled=True),
        (((1,), (1,)), ((), ())),
        preferred_element_type=jnp.float32,
    )
    sigma_out = jnp.transpose(rows_out, (1, 0, 2)).astype(jnp.bfloat16)
    local_gram = jnp.dot(
        left_amps.reshape(root_count, -1),
        sigma_out.reshape(root_count, -1).T,
        preferred_element_type=jnp.float32,
    )
    factor = 1.0 / math.sqrt(OCC_PAIRS * ab_cols * lax.axis_size("pq"))
    subspace = lax.psum(local_gram, ("pq", "hh")) * factor
    return (sigma_out, subspace)


def solution(mesh):
    return jax.shard_map(
        body,
        mesh=mesh,
        in_specs=(P("hh", "pq"), P("hh", "pq"), P(None, "hh", "pq")),
        out_specs=(P(None, "hh", "pq"), P()),
        check_vma=False,
    )
```

profile of v0, /device:TPU:10, one launch (start us, length us, event | category | flops | bytes accessed | tf_op | source)
XLA Modules:
  0.0 574.5 jit_solution(7617182189609885000)
XLA Ops:
  7.2 0.0 copy-start
  7.2 0.0 all-gather.4.cloned.1.call-start
  7.2 0.7 all-gather.4.cloned.1.call-update
  7.9 0.0 reduce-scatter.2.cloned.1.call-start
  8.0 25.3 %all-gather.4.cloned.1.call-done = bf16[4096,256]{1,0:T(8,128)(2,1)} async-done(((bf16[1024,256]{1,0:T(8,128)(2,1)}), bf16[4096,256]{1,0:T(8,128)(2,1)}) %all-gather.4.cloned.1.call-update) | async-done | bytes 2097168 | tf_op jit(solution)/shard_map/all_gather | solution.py:15
  33.3 0.0 copy-done
  33.3 9.7 %fusion.12 = f32[1024,4096]{1,0:T(8,128)} fusion(bf16[1024,256]{1,0:T(8,128)(2,1)S(1)} %copy-done, bf16[4096,256]{1,0:T(8,128)(2,1)} %all-gather.4.cloned.1.call-done), kind=kOutput, calls=%fused_computation.8 | convolution fusion | flops 2147483648 | bytes 19398656 | tf_op jit(solution)/shard_map/dot_general | solution.py:13
  43.0 0.0 reduce-scatter.2.cloned.1.call-update
  43.0 0.0 all-gather.8.cloned.1.call-start
  43.1 0.7 all-gather.8.cloned.1.call-update
  43.7 0.0 all-gather.6.cloned.1.call-start
  43.8 278.5 %reduce-scatter.2.cloned.1.call-done = f32[1024,512]{1,0:T(8,128)} async-done(((f32[1024,4096]{1,0:T(8,128)}), f32[1024,512]{1,0:T(8,128)}) %reduce-scatter.2.cloned.1.call-update) | async-done | bytes 2097168 | tf_op jit(solution)/shard_map/reduce_scatter | solution.py:19
  322.3 2.7 convert_element_type.9
  325.0 0.0 all-gather.6.cloned.1.call-update
  325.1 0.0 copy-start.1
  325.1 57.3 %all-gather.8.cloned.1.call-done = bf16[8,4096,128]{2,1,0:T(8,128)(2,1)} async-done(((bf16[8,1024,128]{2,1,0:T(8,128)(2,1)}), bf16[8,4096,128]{2,1,0:T(8,128)(2,1)}) %all-gather.8.cloned.1.call-update) | async-done | bytes 8388624 | tf_op jit(solution)/shard_map/all_gather | solution.py:25
  382.3 124.7 %all-gather.6.cloned.1.call-done = bf16[1024,4096]{1,0:T(8,128)(2,1)} async-done(((bf16[1024,512]{1,0:T(8,128)(2,1)}), bf16[1024,4096]{1,0:T(8,128)(2,1)}) %all-gather.6.cloned.1.call-update) | async-done | bytes 8388624 | tf_op jit(solution)/shard_map/all_gather | solution.py:22
  507.0 13.7 %convert_bitcast_fusion = bf16[8,1024,128]{2,1,0:T(8,128)(2,1)S(1)} fusion(bf16[8,4096,128]{2,1,0:T(8,128)(2,1)} %all-gather.8.cloned.1.call-done, bf16[1024,4096]{1,0:T(8,128)(2,1)} %all-gather.6.cloned.1.call-done), kind=kOutput, calls=%fused_computation.5 | convolution fusion | flops 8590983168 | bytes 18874368 | tf_op jit(solution)/shard_map/dot_general | solution.py:23
  520.7 0.0 copy-start.2
  520.7 1.3 copy-done.2
  522.0 0.0 copy-done.1
  522.0 2.5 fusion.7
  524.5 42.8 %psum.7 = f32[8,8]{0,1:T(8,128)S(1)} all-reduce(f32[8,8]{0,1:T(8,128)S(1)} %fusion.7), channel_id=1, replica_groups=mesh['pq'=8,'hh'=4] {'pq','hh'}, use_global_device_ids=true, to_apply=%region_1.0 | all-reduce | flops 64 | bytes 512 | tf_op jit(solution)/shard_map/psum | solution.py:36
  567.3 0.7 copy.7
  (1 shorter events, 0.0 us)
Async XLA Ops:
  7.2 26.1 %copy-start = (bf16[1024,256]{1,0:T(8,128)(2,1)S(1)}, bf16[1024,256]{1,0:T(8,128)(2,1)}, u32[]{:S(2)}) copy-start(bf16[1024,256]{1,0:T(8,128)(2,1)} %param.4) | copy-start | bytes 1572868
  7.2 26.1 %all-gather.4.cloned.1.call-start = ((), (), s32[]{:S(2)}) async-start(), calls=%async_computation.1 | async-start | bytes 2621440 | tf_op jit(solution)/shard_map/all_gather | solution.py:15
  7.9 314.4 %reduce-scatter.2.cloned.1.call-start = ((), (), s32[]{:S(2)}) async-start(), calls=%async_computation.2 | async-start | bytes 18874368 | tf_op jit(solution)/shard_map/reduce_scatter | solution.py:19
  43.0 339.3 %all-gather.8.cloned.1.call-start = ((), (), s32[]{:S(2)}) async-start(), calls=%async_computation.4 | async-start | bytes 10485760 | tf_op jit(solution)/shard_map/all_gather | solution.py:25
  43.7 463.3 %all-gather.6.cloned.1.call-start = ((), (), s32[]{:S(2)}) async-start(), calls=%async_computation.3 | async-start | bytes 9437184 | tf_op jit(solution)/shard_map/all_gather | solution.py:22
  325.1 196.9 %copy-start.1 = (bf16[8,1024,128]{2,1,0:T(8,128)(2,1)S(1)}, bf16[8,1024,128]{2,1,0:T(8,128)(2,1)}, u32[]{:S(2)}) copy-start(bf16[8,1024,128]{2,1,0:T(8,128)(2,1)} %param.5) | copy-start | bytes 6291460
  520.7 1.3 copy-start.2
Sparse Core Ops, SparseCore 0:
  9.5 23.6 all-gather.3
  43.1 279.1 reduce-scatter.1
  323.9 58.3 all-gather.7
  384.8 122.1 all-gather.5
where the time goes:
time: 575 us; the launch traced here: 574 us
  waiting for transfers between devices  487 us (85%)
  blocking collectives  42.8 us (7%)
  matrix products  25.9 us (5%)
  between operations  13.8 us (2%)
    reduce_scatter x1, waiting for transfers between devices, body(): lax.psum_scatter(partial_t, 'pq', scatter_dimension=1, tiled=True)  279 us
    all_gather x1, waiting for transfers between devices, body(): ladder_t = lax.all_gather(ladder_t, 'pq', axis=1, tiled=True)  125 us
    all_gather x1, waiting for transfers between devices, body(): lax.all_gather(left_amps, 'hh', axis=1, tiled=True)  57.3 us
    psum x1, blocking collectives, body(): subspace = lax.psum(local_gram, ('pq', 'hh')) * factor  42.8 us
    all_gather x1, waiting for transfers between devices, body(): lax.all_gather(amplitudes, 'hh', axis=0, tiled=True)  25.3 us
    dot_general x1, matrix products, body(): lax.dot_general(ladder_t, lax.all_gather(left_amps, 'hh', axis=1, tiled=T...  13.7 us
  transfers between devices with their start and end apart: 4, of which 4 were waited for; matrix products, arithmetic and copies ran while one was open for 0% of the time, Pallas kernels for 0%

commit v1 on v0

--- a/solution.py
+++ b/solution.py
@@ -33,7 +33,7 @@
         preferred_element_type=jnp.float32,
     )
     factor = 1.0 / math.sqrt(OCC_PAIRS * ab_cols * lax.axis_size("pq"))
-    subspace = lax.psum(local_gram, ("pq", "hh")) * factor
+    subspace = lax.psum(lax.psum(local_gram, "hh"), "pq") * factor
     return (sigma_out, subspace)
 
 

time: 575 us -> 562 us (0.977); the launches traced: 574 us -> 555 us
  blocking collectives: 42.8 us -> 23.6 us
    psum x1 -> x2, blocking collectives: 42.8 us -> 23.6 us  [body(): subspace = lax.psum(lax.psum(local_gram, 'hh'), 'pq') * factor]
where the time goes in v1:
time: 562 us; the launch traced here: 555 us
  waiting for transfers between devices  487 us (87%)
  matrix products  25.9 us (5%)
  blocking collectives  23.6 us (4%)
  between operations  13.8 us (2%)
    reduce_scatter x1, waiting for transfers between devices, body(): lax.psum_scatter(partial_t, 'pq', scatter_dimension=1, tiled=True)  279 us
    all_gather x1, waiting for transfers between devices, body(): ladder_t = lax.all_gather(ladder_t, 'pq', axis=1, tiled=True)  125 us
    all_gather x1, waiting for transfers between devices, body(): lax.all_gather(left_amps, 'hh', axis=1, tiled=True)  57.3 us
    all_gather x1, waiting for transfers between devices, body(): lax.all_gather(amplitudes, 'hh', axis=0, tiled=True)  25.3 us
    psum x2, blocking collectives, body(): subspace = lax.psum(lax.psum(local_gram, 'hh'), 'pq') * factor  23.6 us
    dot_general x1, matrix products, body(): lax.dot_general(ladder_t, lax.all_gather(left_amps, 'hh', axis=1, tiled=T...  13.7 us
  transfers between devices with their start and end apart: 4, of which 4 were waited for; matrix products, arithmetic and copies ran while one was open for 0% of the time, Pallas kernels for 0%

profile of v1, /device:TPU:10, one launch (start us, length us, event | category | flops | bytes accessed | tf_op | source)
XLA Modules:
  0.0 555.3 jit_solution(4055228888567046507)
XLA Ops:
  7.2 0.0 copy-start
  7.2 0.0 all-gather.4.cloned.1.call-start
  7.2 0.7 all-gather.4.cloned.1.call-update
  7.9 0.0 reduce-scatter.2.cloned.1.call-start
  8.0 25.3 %all-gather.4.cloned.1.call-done = bf16[4096,256]{1,0:T(8,128)(2,1)} async-done(((bf16[1024,256]{1,0:T(8,128)(2,1)}), bf16[4096,256]{1,0:T(8,128)(2,1)}) %all-gather.4.cloned.1.call-update) | async-done | bytes 2097168 | tf_op jit(solution)/shard_map/all_gather | solution.py:15
  33.3 0.0 copy-done
  33.3 9.7 %fusion.12 = f32[1024,4096]{1,0:T(8,128)} fusion(bf16[1024,256]{1,0:T(8,128)(2,1)S(1)} %copy-done, bf16[4096,256]{1,0:T(8,128)(2,1)} %all-gather.4.cloned.1.call-done), kind=kOutput, calls=%fused_computation.8 | convolution fusion | flops 2147483648 | bytes 19398656 | tf_op jit(solution)/shard_map/dot_general | solution.py:13
  43.0 0.0 reduce-scatter.2.cloned.1.call-update
  43.0 0.0 all-gather.8.cloned.1.call-start
  43.1 0.7 all-gather.8.cloned.1.call-update
  43.7 0.0 all-gather.6.cloned.1.call-start
  43.8 278.5 %reduce-scatter.2.cloned.1.call-done = f32[1024,512]{1,0:T(8,128)} async-done(((f32[1024,4096]{1,0:T(8,128)}), f32[1024,512]{1,0:T(8,128)}) %reduce-scatter.2.cloned.1.call-update) | async-done | bytes 2097168 | tf_op jit(solution)/shard_map/reduce_scatter | solution.py:19
  322.3 2.7 convert_element_type.9
  325.0 0.0 all-gather.6.cloned.1.call-update
  325.1 0.0 copy-start.1
  325.1 57.3 %all-gather.8.cloned.1.call-done = bf16[8,4096,128]{2,1,0:T(8,128)(2,1)} async-done(((bf16[8,1024,128]{2,1,0:T(8,128)(2,1)}), bf16[8,4096,128]{2,1,0:T(8,128)(2,1)}) %all-gather.8.cloned.1.call-update) | async-done | bytes 8388624 | tf_op jit(solution)/shard_map/all_gather | solution.py:25
  382.3 124.7 %all-gather.6.cloned.1.call-done = bf16[1024,4096]{1,0:T(8,128)(2,1)} async-done(((bf16[1024,512]{1,0:T(8,128)(2,1)}), bf16[1024,4096]{1,0:T(8,128)(2,1)}) %all-gather.6.cloned.1.call-update) | async-done | bytes 8388624 | tf_op jit(solution)/shard_map/all_gather | solution.py:22
  507.0 13.7 %convert_bitcast_fusion = bf16[8,1024,128]{2,1,0:T(8,128)(2,1)S(1)} fusion(bf16[8,4096,128]{2,1,0:T(8,128)(2,1)} %all-gather.8.cloned.1.call-done, bf16[1024,4096]{1,0:T(8,128)(2,1)} %all-gather.6.cloned.1.call-done), kind=kOutput, calls=%fused_computation.5 | convolution fusion | flops 8590983168 | bytes 18874368 | tf_op jit(solution)/shard_map/dot_general | solution.py:23
  520.7 0.0 copy-start.2
  520.7 1.3 copy-done.2
  522.0 0.0 copy-done.1
  522.0 2.5 fusion.7
  524.5 5.8 %psum.14 = f32[8,8]{0,1:T(8,128)S(1)} all-reduce(f32[8,8]{0,1:T(8,128)S(1)} %fusion.7), channel_id=1, replica_groups=mesh['pq'=8,'hh'=4] {'hh'}, use_global_device_ids=true, to_apply=%region_1.0 | all-reduce | flops 64 | bytes 512 | tf_op jit(solution)/shard_map/psum | solution.py:36
  530.4 17.8 %psum.15 = f32[8,8]{0,1:T(8,128)S(1)} all-reduce(f32[8,8]{0,1:T(8,128)S(1)} %psum.14), channel_id=1, replica_groups=mesh['pq'=8,'hh'=4] {'pq'}, use_global_device_ids=true, to_apply=%region_2.0 | all-reduce | flops 64 | bytes 512 | tf_op jit(solution)/shard_map/psum | solution.py:36
  548.1 0.7 copy.7
  (1 shorter events, 0.0 us)
Async XLA Ops:
  7.2 26.1 %copy-start = (bf16[1024,256]{1,0:T(8,128)(2,1)S(1)}, bf16[1024,256]{1,0:T(8,128)(2,1)}, u32[]{:S(2)}) copy-start(bf16[1024,256]{1,0:T(8,128)(2,1)} %param.4) | copy-start | bytes 1572868
  7.2 26.1 %all-gather.4.cloned.1.call-start = ((), (), s32[]{:S(2)}) async-start(), calls=%async_computation.1 | async-start | bytes 2621440 | tf_op jit(solution)/shard_map/all_gather | solution.py:15
  7.9 314.4 %reduce-scatter.2.cloned.1.call-start = ((), (), s32[]{:S(2)}) async-start(), calls=%async_computation.2 | async-start | bytes 18874368 | tf_op jit(solution)/shard_map/reduce_scatter | solution.py:19
  43.0 339.3 %all-gather.8.cloned.1.call-start = ((), (), s32[]{:S(2)}) async-start(), calls=%async_computation.4 | async-start | bytes 10485760 | tf_op jit(solution)/shard_map/all_gather | solution.py:25
  43.7 463.3 %all-gather.6.cloned.1.call-start = ((), (), s32[]{:S(2)}) async-start(), calls=%async_computation.3 | async-start | bytes 9437184 | tf_op jit(solution)/shard_map/all_gather | solution.py:22
  325.1 196.9 %copy-start.1 = (bf16[8,1024,128]{2,1,0:T(8,128)(2,1)S(1)}, bf16[8,1024,128]{2,1,0:T(8,128)(2,1)}, u32[]{:S(2)}) copy-start(bf16[8,1024,128]{2,1,0:T(8,128)(2,1)} %param.5) | copy-start | bytes 6291460
  520.7 1.3 copy-start.2
Sparse Core Ops, SparseCore 0:
  9.5 23.6 all-gather.3
  43.1 279.1 reduce-scatter.1
  323.9 58.3 all-gather.7
  384.8 122.1 all-gather.5

commit v2 on v0

--- a/solution.py
+++ b/solution.py
@@ -22,7 +22,9 @@
     ladder_t = lax.all_gather(ladder_t, "pq", axis=1, tiled=True)
     rows_out = lax.dot_general(
         ladder_t,
-        lax.all_gather(left_amps, "hh", axis=1, tiled=True),
+        jnp.concatenate(
+            lax.all_to_all(jnp.stack([left_amps] * lax.axis_size("hh")), "hh", 0, 0), axis=1
+        ),
         (((1,), (1,)), ((), ())),
         preferred_element_type=jnp.float32,
     )

time: 575 us -> 515 us (0.90)
  waiting for transfers between devices: 487 us -> 321 us
  blocking collectives: 42.8 us -> 140 us
  local copies, waits for them, and re-layouts: 1.99 us -> 11.5 us
    all_gather x1, waiting for transfers between devices: 125 us -> 16 us  [body(): ladder_t = lax.all_gather(ladder_t, 'pq', axis=1, tiled=True)]
    all_to_all x0 -> x1, blocking collectives: none -> 96.9 us  [body(): lax.all_to_all(jnp.stack([left_amps] * lax.axis_size('hh')), 'hh', 0, 0)]
    all_gather x1 -> x0, waiting for transfers between devices: 57.3 us -> none  [body(): lax.all_gather(left_amps, 'hh', axis=1, tiled=True)]
    reshape x0 -> x1, local copies, waits for them, and re-layouts: none -> 7.67 us  [body(): jnp.concatenate(lax.all_to_all(jnp.stack([left_amps] * lax.axis_size('hh'...]
  transfers between devices with their start and end apart: 4 -> 3, of which waited for: 4 -> 3; matrix products, arithmetic and copies ran while one was open for 0% -> 2% of each run, Pallas kernels for 0% -> 0%
where the time goes in v2:
time: 515 us
  waiting for transfers between devices  321 us (62%)
  blocking collectives  140 us (27%)
  matrix products  25.9 us (5%)
  between operations  13.8 us (3%)
  local copies, waits for them, and re-layouts  11.5 us (2%)
    reduce_scatter x1, waiting for transfers between devices, body(): lax.psum_scatter(partial_t, 'pq', scatter_dimension=1, tiled=True)  279 us
    all_to_all x1, blocking collectives, body(): lax.all_to_all(jnp.stack([left_amps] * lax.axis_size('hh')), 'hh', 0, 0)  96.9 us
    psum x1, blocking collectives, body(): subspace = lax.psum(local_gram, ('pq', 'hh')) * factor  42.7 us
    all_gather x1, waiting for transfers between devices, body(): lax.all_gather(amplitudes, 'hh', axis=0, tiled=True)  25.3 us
    all_gather x1, waiting for transfers between devices, body(): ladder_t = lax.all_gather(ladder_t, 'pq', axis=1, tiled=True)  16 us
    dot_general x1, matrix products, body(): lax.dot_general(ladder_t, jnp.concatenate(lax.all_to_all(jnp.stack([left_...  13.7 us
  transfers between devices with their start and end apart: 3, of which 3 were waited for; matrix products, arithmetic and copies ran while one was open for 2% of the time, Pallas kernels for 0%

profile of v2, /device:TPU:10, one launch (start us, length us, event | category | flops | bytes accessed | tf_op | source)
XLA Modules:
  0.0 515.0 jit_solution(2135595707194265119)
XLA Ops:
  7.2 0.0 copy-start
  7.2 0.0 all-gather.3.cloned.1.call-start
  7.2 0.7 all-gather.3.cloned.1.call-update
  7.9 0.0 reduce-scatter.2.cloned.1.call-start
  8.0 25.3 %all-gather.3.cloned.1.call-done = bf16[4096,256]{1,0:T(8,128)(2,1)} async-done(((bf16[1024,256]{1,0:T(8,128)(2,1)}), bf16[4096,256]{1,0:T(8,128)(2,1)}) %all-gather.3.cloned.1.call-update) | async-done | bytes 2097168 | tf_op jit(solution)/shard_map/all_gather | solution.py:15
  33.3 0.0 copy-done
  33.3 9.7 %fusion.12 = f32[1024,4096]{1,0:T(8,128)} fusion(bf16[1024,256]{1,0:T(8,128)(2,1)S(1)} %copy-done, bf16[4096,256]{1,0:T(8,128)(2,1)} %all-gather.3.cloned.1.call-done), kind=kOutput, calls=%fused_computation.8 | convolution fusion | flops 2147483648 | bytes 19398656 | tf_op jit(solution)/shard_map/dot_general | solution.py:13
  43.0 0.0 reduce-scatter.2.cloned.1.call-update
  43.0 0.0 copy-start.1
  43.0 0.0 all-gather.5.cloned.1.call-start
  43.1 279.3 %reduce-scatter.2.cloned.1.call-done = f32[1024,512]{1,0:T(8,128)} async-done(((f32[1024,4096]{1,0:T(8,128)}), f32[1024,512]{1,0:T(8,128)}) %reduce-scatter.2.cloned.1.call-update) | async-done | bytes 2097168 | tf_op jit(solution)/shard_map/reduce_scatter | solution.py:19
  322.3 2.7 convert_element_type.9
  325.0 0.0 all-gather.5.cloned.1.call-update
  325.1 0.0 copy-done.1
  325.1 1.9 stack.2
  326.9 96.9 %all_to_all.5 = bf16[4,8,1024,128]{3,2,1,0:T(8,128)(2,1)} all-to-all(bf16[4,8,1024,128]{3,2,1,0:T(8,128)(2,1)S(1)} %stack.2), channel_id=1, replica_groups=mesh['pq'=8,'hh'=4] {'hh'}, dimensions={0} | all-to-all | bytes 16777216 | tf_op jit(solution)/shard_map/all_to_all | solution.py:26
  423.8 7.7 %copy.8 = bf16[8,4,1024,128]{3,2,1,0:T(8,128)(2,1)} copy(bf16[8,4,1024,128]{3,2,0,1:T(8,128)(2,1)} %bitcast.16) | data formatting | bytes 16777216 | tf_op jit(solution)/shard_map/reshape | solution.py:25
  431.5 16.0 %all-gather.5.cloned.1.call-done = bf16[1024,4096]{1,0:T(8,128)(2,1)} async-done(((bf16[1024,512]{1,0:T(8,128)(2,1)}), bf16[1024,4096]{1,0:T(8,128)(2,1)}) %all-gather.5.cloned.1.call-update) | async-done | bytes 8388624 | tf_op jit(solution)/shard_map/all_gather | solution.py:22
  447.5 13.7 %convert_bitcast_fusion = bf16[8,1024,128]{2,1,0:T(8,128)(2,1)S(1)} fusion(bf16[8,4096,128]{2,1,0:T(8,128)(2,1)} %bitcast.17, bf16[1024,4096]{1,0:T(8,128)(2,1)} %all-gather.5.cloned.1.call-done), kind=kOutput, calls=%fused_computation.5 | convolution fusion | flops 8590983168 | bytes 18874368 | tf_op jit(solution)/shard_map/dot_general | solution.py:23
  461.2 0.0 copy-start.2
  461.2 1.3 copy-done.2
  462.5 2.5 fusion.7
  465.0 42.7 %psum.7 = f32[8,8]{0,1:T(8,128)S(1)} all-reduce(f32[8,8]{0,1:T(8,128)S(1)} %fusion.7), channel_id=1, replica_groups=mesh['pq'=8,'hh'=4] {'pq','hh'}, use_global_device_ids=true, to_apply=%region_1.0 | all-reduce | flops 64 | bytes 512 | tf_op jit(solution)/shard_map/psum | solution.py:38
  507.8 0.7 copy.11
  (1 shorter events, 0.0 us)
Async XLA Ops:
  7.2 26.1 %copy-start = (bf16[1024,256]{1,0:T(8,128)(2,1)S(1)}, bf16[1024,256]{1,0:T(8,128)(2,1)}, u32[]{:S(2)}) copy-start(bf16[1024,256]{1,0:T(8,128)(2,1)} %param.4) | copy-start | bytes 1572868
  7.2 26.1 %all-gather.3.cloned.1.call-start = ((), (), s32[]{:S(2)}) async-start(), calls=%async_computation.2 | async-start | bytes 2621440 | tf_op jit(solution)/shard_map/all_gather | solution.py:15
  7.9 314.4 %reduce-scatter.2.cloned.1.call-start = ((), (), s32[]{:S(2)}) async-start(), calls=%async_computation.3 | async-start | bytes 18874368 | tf_op jit(solution)/shard_map/reduce_scatter | solution.py:19
  43.0 282.0 %copy-start.1 = (bf16[8,1024,128]{2,1,0:T(8,128)(2,1)S(1)}, bf16[8,1024,128]{2,1,0:T(8,128)(2,1)}, u32[]{:S(2)}) copy-start(bf16[8,1024,128]{2,1,0:T(8,128)(2,1)} %param.5) | copy-start | bytes 6291460
  43.0 404.5 %all-gather.5.cloned.1.call-start = ((), (), s32[]{:S(2)}) async-start(), calls=%async_computation.4 | async-start | bytes 9437184 | tf_op jit(solution)/shard_map/all_gather | solution.py:22
  461.2 1.3 copy-start.2
Sparse Core Ops, SparseCore 0:
  9.5 23.6 all-gather.2
  43.1 279.1 reduce-scatter.1
  325.2 122.2 all-gather.4
